TPU v7x, 32 devices: a whole 2x2x4 slice. The times are simulated.
32 devices in a mesh: row: 8 (over z, y), col: 4 (over x, core).
Axes of the slice: x: 2, y: 2, z: 4, core: 2. Of those that a mesh axis runs over, the one named last changes fastest.
Arguments:
- eigvec_halves: float32 [1536, 32768], P('col', 'row'), may hold values from -6 to 6
- rotation_mate: int32 [1536], replicated, may hold values from 0 to 1535, as said below
- givens_theta: float32 [1536], replicated, may hold values from -3.140625 to 3.140625
- kept_vectors: int32 [1536], replicated, may hold values from 0 to 1535, as said below
- secular_singularities: float32 [1536], replicated, may hold values from -0.25 to 1535.25, as said below
- secular_coefficients: float32 [1536], replicated, may hold values from -6 to 6
- secular_zeros: float32 [512], replicated, may hold values from 0.4 to 1535.6
Outputs:
- packed_vectors: float32 [1536, 32768], P(('row', 'col'))
- panel: float32 [512, 32768], P('col', 'row')
Inputs may be any that keep to these rules, and one draw needn't show every extreme that they name: `rotation_mate`: partner is an involution. Column blocks of 384 belong to the indices of col in order; at most 24 columns of one block pair with columns of any one other block, exactly that many for some two blocks in every draw. `kept_vectors`: survivors is a permutation. Compacted positions form consecutive blocks of 48, one block per device of row+col in order; one block takes at most 16 columns from any one column block of 384, exactly that many from some. secular_singularities[k] lies within 0.25 of k.
All inputs are finite; a program needn't handle non-finite values.
Results may differ from a plain program's by a relative error of at most 0.00007.
Values sent between devices are 32-bit elements; how exact they have to be, the bound alone decides.
A program may use at most 128 MiB of HBM per device.

v0:
```python
import jax
import jax.numpy as jnp
from jax import lax
from jax.sharding import PartitionSpec as P


def rank_within(groups, member, group_count):
    onehot = (
        (groups[:, None] == jnp.arange(group_count, dtype=jnp.int32)[None, :]) & member[:, None]
    ).astype(jnp.int32)
    before = jnp.cumsum(onehot, axis=0) - onehot
    return jnp.sum(before * onehot, axis=1)


def bucket_table(sort_keys, boundary_keys, capacity):
    ordering = jnp.argsort(sort_keys, stable=True)
    sorted_keys = sort_keys[ordering]
    edge_ids = jnp.searchsorted(sorted_keys, boundary_keys)
    slot_ids = jnp.arange(capacity, dtype=jnp.int32)
    usable = slot_ids[None, :] < (edge_ids[1:] - edge_ids[:-1])[:, None]
    picked = jnp.where(usable, edge_ids[:-1, None] + slot_ids[None, :], 0)
    return (ordering[picked], usable)


def selector(index_list, valid, source_count):
    sources = jnp.arange(source_count, dtype=jnp.int32)[None, :]
    return ((index_list[:, None] == sources) & valid[:, None]).astype(jnp.float32)


def select_rows(index_list, valid, source):
    pick = selector(index_list, valid, source.shape[0])
    return jnp.dot(
        pick, source, precision=lax.Precision.HIGHEST, preferred_element_type=jnp.float32
    )


def shards(
    eigvec_halves,
    rotation_mate,
    givens_theta,
    kept_vectors,
    secular_singularities,
    secular_coefficients,
    secular_zeros,
):
    col_count = lax.axis_size("col")
    row_count = lax.axis_size("row")
    block_cols, block_rows = eigvec_halves.shape
    total_cols = rotation_mate.shape[0]
    panel_cols = secular_zeros.shape[0]
    pair_cap = block_cols // 16
    col_index = lax.axis_index("col")
    first_col = col_index * block_cols
    local_labels = first_col + jnp.arange(block_cols, dtype=jnp.int32)
    mate_ids = lax.dynamic_slice_in_dim(rotation_mate, first_col, block_cols)
    paired = mate_ids != local_labels
    owner_col = mate_ids // block_cols
    remote = paired & (owner_col != col_index)
    pair_keys = jnp.where(remote, owner_col * total_cols + mate_ids, col_count * total_cols)
    pair_edges = jnp.arange(col_count + 1, dtype=jnp.int32) * total_cols
    chosen, usable = bucket_table(pair_keys, pair_edges, pair_cap)
    outgoing = select_rows(chosen.reshape(-1), usable.reshape(-1), eigvec_halves).reshape(
        col_count, pair_cap, block_rows
    )
    incoming = lax.all_to_all(outgoing, "col", split_axis=0, concat_axis=0, tiled=True)
    rank_here = rank_within(owner_col, remote, col_count)
    flat_in = incoming.reshape(col_count * pair_cap, block_rows)
    from_remote = select_rows(owner_col * pair_cap + rank_here, remote, flat_in)
    from_local = select_rows(mate_ids - first_col, paired & jnp.logical_not(remote), eigvec_halves)
    mate_rows = from_remote + from_local
    angles_here = givens_theta[jnp.minimum(local_labels, mate_ids)]
    sign_flip = jnp.where(local_labels < mate_ids, -1.0, 1.0).astype(jnp.float32)
    cosine = jnp.where(paired, jnp.cos(angles_here), 1.0)
    sine_term = jnp.where(paired, sign_flip * jnp.sin(angles_here), 0.0)
    spun_vectors = cosine[:, None] * eigvec_halves + sine_term[:, None] * mate_rows
    spot_sequence = jnp.argsort(kept_vectors)[local_labels]
    cauchy_raw = secular_coefficients[spot_sequence][:, None] / (
        secular_singularities[spot_sequence][:, None] - secular_zeros[None, :]
    )

    def add_block(block_index, running):
        pole_block = lax.dynamic_slice_in_dim(
            secular_singularities, block_index * block_cols, block_cols
        )
        weight_block = lax.dynamic_slice_in_dim(
            secular_coefficients, block_index * block_cols, block_cols
        )
        block_raw = weight_block[:, None] / (pole_block[:, None] - secular_zeros[None, :])
        return running + jnp.sum(block_raw * block_raw, axis=0)

    col_sq = lax.fori_loop(0, col_count, add_block, jnp.zeros((panel_cols,), jnp.float32))
    cauchy = cauchy_raw * lax.rsqrt(col_sq + 1e-06)[None, :]
    panel = lax.psum_scatter(
        lax.dot_general(
            cauchy,
            spun_vectors,
            (((0,), (0,)), ((), ())),
            precision=lax.Precision.HIGHEST,
            preferred_element_type=jnp.float32,
        ),
        "col",
        scatter_dimension=0,
        tiled=True,
    )
    dest_count = row_count * col_count
    every_destination = block_cols // row_count
    share_base = every_destination // col_count
    move_cap = share_base + share_base // 3
    move_edges = jnp.arange(dest_count + 1, dtype=jnp.int32) * every_destination
    chosen_move, usable_move = bucket_table(spot_sequence, move_edges, move_cap)
    parcels = select_rows(chosen_move.reshape(-1), usable_move.reshape(-1), spun_vectors).reshape(
        dest_count, move_cap, block_rows
    )
    arrived = lax.all_to_all(parcels, ("row", "col"), split_axis=0, concat_axis=0, tiled=True)
    arrived = arrived.reshape(row_count, col_count * move_cap, block_rows)
    destination_slot = lax.axis_index("row") * col_count + col_index
    wanted_vectors = lax.dynamic_slice_in_dim(
        kept_vectors, destination_slot * every_destination, every_destination
    )
    source_col = wanted_vectors // block_cols
    source_rank = rank_within(source_col, jnp.ones(source_col.shape, dtype=jnp.bool_), col_count)
    final_pick = selector(
        source_col * move_cap + source_rank,
        jnp.ones(source_col.shape, dtype=jnp.bool_),
        col_count * move_cap,
    )
    placed = lax.dot_general(
        final_pick,
        arrived,
        (((1,), (1,)), ((), ())),
        precision=lax.Precision.HIGHEST,
        preferred_element_type=jnp.float32,
    )
    packed_vectors = placed.reshape(every_destination, row_count * block_rows)
    return (packed_vectors, panel)


def solution(mesh):
    placed = (P("col", "row"), P(), P(), P(), P(), P(), P())
    return jax.shard_map(
        shards,
        mesh=mesh,
        in_specs=placed,
        out_specs=(P(("row", "col"), None), P("col", "row")),
        check_vma=False,
    )
```

profile of v0, /device:TPU:0, one launch (start us, length us, event | category | flops | bytes accessed | tf_op | source)
XLA Modules:
  0.0 304.1 jit_solution(18356329492080307266)
XLA Ops:
  7.2 0.8 not_and_fusion
  8.0 1.2 reduce-window.6
  9.2 0.2 slice_reduce_fusion
  9.5 0.2 reduce-window.9
  9.7 0.8 broadcast_subtract_fusion
  10.5 3.8 %sort.50 = (s32[384]{0:T(512)}, s32[384]{0:T(512)S(1)}) sort(s32[384]{0:T(512)S(1)} %get-tuple-element.322, s32[384]{0:T(512)S(1)} %iota.74), dimensions={0}, to_apply=%region_9.10 | sort | flops 3456 | bytes 6144 | tf_op jit(solution)/shard_map/jit(argsort)/sort | solution.py:16
  14.3 2.8 gather_fusion.6
  17.1 6.3 %while.63 = (s32[]{:T(128)}, u32[5]{0:T(128)S(1)}, u32[5]{0:T(128)S(1)}, s32[384]{0:T(512)S(1)}, s32[]{:T(128)}, /*index=5*/s32[]{:T(128)}, s32[]{}) while((s32[]{:T(128)}, u32[5]{0:T(128)S(1)}, u32[5]{0:T(128)S(1)}, s32[384]{0:T(512)S(1)}, s32[]{:T(128)}, /*index=5*/s32[]{:T(128)}, s32[]{}) %tuple.101), condition=%wide.region_11.12_spmd.clone, body=%wide.region_10.11_spmd.clone.sunk | while | flops 1098 | bytes 4436 | solution.py:18
  17.2 0.6 gather_fusion.1
  17.9 0.6 gather_fusion.1
  18.6 0.6 gather_fusion.1
  19.3 0.6 gather_fusion.1
  20.0 0.6 gather_fusion.1
  20.7 0.6 gather_fusion.1
  21.4 0.6 gather_fusion.1
  22.1 0.6 gather_fusion.1
  22.8 0.6 gather_fusion.1
  23.5 0.1 iota_compare_fusion.11
  23.6 0.1 lt.178
  23.8 0.1 reshape.323
  23.9 1.3 gather_fusion.7
  25.2 6.5 %fusion.29 = f32[96,4096]{1,0:T(8,128)} fusion(f32[384,4096]{1,0:T(8,128)} %param.13, s32[96]{0:T(128)S(1)} %gather_fusion.7, pred[96]{0:T(512)(128)(4,1)S(1)} %lt.178), kind=kOutput, calls=%fused_computation.51 | convolution fusion | flops 1812013056 | bytes 7864800 | tf_op jit(solution)/shard_map/dot_general | solution.py:32
  31.7 4.3 %all-to-all-start = ((f32[4,24,4096]{2,1,0:T(8,128)}), f32[4,24,4096]{2,1,0:T(8,128)}, u32[]{:S(2)}, u32[]{:S(2)}) async-start(f32[4,24,4096]{2,1,0:T(8,128)} %bitcast.3), calls=%async_computation | async-start | bytes 3145728 | tf_op jit(solution)/shard_map/all_to_all | solution.py:65
  36.2 1.6 while.64
  36.2 0.1 dynamic_slice.37
  36.3 0.2 multiply_reduce_fusion.2
  36.6 0.1 dynamic_slice.37
  36.8 0.2 multiply_reduce_fusion.2
  37.0 0.1 dynamic_slice.37
  37.2 0.2 multiply_reduce_fusion.2
  37.4 0.1 dynamic_slice.37
  37.6 0.2 multiply_reduce_fusion.2
  37.8 5.0 %sort.48 = (s32[1536]{0:T(1024)}, s32[1536]{0:T(1024)S(1)}) sort(s32[1536]{0:T(1024)S(1)} %copy-done.5, s32[1536]{0:T(1024)S(1)} %iota.69), dimensions={0}, to_apply=%region_2.3 | sort | flops 16896 | bytes 24576 | tf_op jit(solution)/shard_map/jit(argsort)/sort | solution.py:76
  42.9 2.5 gather_fusion.2
  45.4 3.8 %sort.49 = (s32[384]{0:T(512)}, s32[384]{0:T(512)S(1)}) sort(s32[384]{0:T(512)S(1)} %gather_fusion.2, s32[384]{0:T(512)S(1)} %iota.71), dimensions={0}, to_apply=%region_3.4 | sort | flops 3456 | bytes 6144 | tf_op jit(solution)/shard_map/jit(argsort)/sort | solution.py:16
  49.2 2.8 gather_fusion.3
  52.0 7.7 %while.62 = (s32[]{:T(128)}, u32[33]{0:T(128)S(1)}, u32[33]{0:T(128)S(1)}, s32[384]{0:T(512)S(1)}, s32[]{:T(128)}, /*index=5*/s32[]{:T(128)}, s32[]{}) while((s32[]{:T(128)}, u32[33]{0:T(128)S(1)}, u32[33]{0:T(128)S(1)}, s32[384]{0:T(512)S(1)}, s32[]{:T(128)}, /*index=5*/s32[]{:T(128)}, s32[]{}) %tuple.104), condition=%wide.region_5.6_spmd.clone, body=%wide.region_4.5_spmd.clone.sunk | while | flops 1490 | bytes 5780 | solution.py:18
  52.1 0.8 gather_fusion
  52.9 0.8 gather_fusion
  53.8 0.8 gather_fusion
  54.6 0.8 gather_fusion
  55.5 0.8 gather_fusion
  56.3 0.8 gather_fusion
  57.2 0.8 gather_fusion
  58.0 0.8 gather_fusion
  58.9 0.8 gather_fusion
  59.8 2.5 gather_fusion.9
  62.3 2.5 gather_fusion.8
  64.9 0.1 lt.165
  65.1 0.1 reshape.299
  65.2 3.5 %gather_fusion.4 = s32[512]{0:T(512)S(1)} fusion(s32[384]{0:T(512)S(1)} %get-tuple-element.230, s32[1024]{0:T(1024)S(1)} %pad_clamp_fusion.6), kind=kCustom, calls=%fused_computation.4 | custom fusion | bytes 6144 | tf_op jit(solution)/shard_map/gather | solution.py:22
  68.7 2.7 gather_fusion.5
  71.5 0.8 cosine_select_fusion
  72.2 4.3 %fusion.26 = f32[384,4096]{1,0:T(8,128)S(1)} fusion(f32[96,4096]{1,0:T(8,128)} %bitcast.4, s32[384]{0:T(512)S(1)} %get-tuple-element.326, pred[384]{0:T(512)(128)(4,1)S(1)} %get-tuple-element.314), kind=kOutput, calls=%fused_computation.48 | convolution fusion | flops 1812013056 | bytes 7866240 | tf_op jit(solution)/shard_map/dot_general | solution.py:32
  76.6 6.5 %multiply_add_fusion = f32[384,4096]{1,0:T(8,128)S(1)} fusion(f32[384,4096]{1,0:T(8,128)S(1)} %fusion.26, f32[384,4096]{1,0:T(8,128)S(1)} %bitcast.42, f32[384]{0:T(512)S(1)} %get-tuple-element.325, f32[384]{0:T(512)S(1)} %get-tuple-element.324, s32[384]{0:T(512)S(1)} %get-tuple-element.321, pred[384]{0:T(512)(128)(4,1)S(1)} %get-tuple-element.313), kind=kOutput, calls=%fused_computation.28 | convolution fusion | flops 7254343680 | bytes 18879360 | tf_op jit(solution)/shard_map/dot_general | solution.py:32
  83.1 9.1 %fusion.13 = f32[512,4096]{1,0:T(8,128)} fusion(f32[384,4096]{1,0:T(8,128)S(1)} %multiply_add_fusion, s32[512]{0:T(512)S(1)} %gather_fusion.4, pred[512]{0:T(512)(128)(4,1)S(1)} %lt.165), kind=kOutput, calls=%fused_computation.35 | convolution fusion | flops 9664069632 | bytes 14682624 | tf_op jit(solution)/shard_map/dot_general | solution.py:32
  92.2 7.9 %all-to-all-start.1 = ((f32[32,16,4096]{2,1,0:T(8,128)}), f32[32,16,4096]{2,1,0:T(8,128)}, u32[]{:S(2)}, u32[]{:S(2)}) async-start(f32[32,16,4096]{2,1,0:T(8,128)} %bitcast.39), calls=%async_computation.1 | async-start | bytes 16777216 | tf_op jit(solution)/shard_map/all_to_all | solution.py:114
  100.2 18.0 %fusion.8 = f32[512,4096]{1,0:T(8,128)} fusion(f32[384,4096]{1,0:T(8,128)} %copy-done.3, f32[512]{0:T(512)S(1)} %add_rsqrt_fusion, f32[512]{0:T(512)S(1)} %get-tuple-element.496, f32[384]{0:T(512)S(1)} %gather_fusion.9, f32[384]{0:T(512)S(1)} %gather_fusion.8), kind=kOutput, calls=%fused_computation.29 | convolution fusion | flops 9664266240 | bytes 14687232 | tf_op jit(solution)/shard_map/dot_general | solution.py:94
  118.2 0.1 and_select_fusion
  118.5 0.2 select_reduce_fusion
  118.7 0.1 multiply_add_fusion.2
  118.7 168.7 %all-to-all-done.1 = f32[32,16,4096]{2,1,0:T(8,128)} async-done(((f32[32,16,4096]{2,1,0:T(8,128)}), f32[32,16,4096]{2,1,0:T(8,128)}, u32[]{:S(2)}, u32[]{:S(2)}) %all-to-all-start.1) | async-done | bytes 8388640 | tf_op jit(solution)/shard_map/all_to_all | solution.py:114
  287.5 3.9 %copy.11 = f32[8,8,8,4096]{3,2,0,1:T(8,128)S(1)} copy(f32[8,8,8,4096]{3,2,1,0:T(8,128)} %bitcast.9) | data formatting | bytes 16777216 | tf_op jit(solution)/shard_map/dot_general | solution.py:127
  291.4 5.9 %fusion.36 = f32[48,32768]{1,0:T(8,128)} fusion(f32[32768,64]{0,1:T(8,128)S(1)} %bitcast.40, s32[48]{0:T(128)S(1)} %multiply_add_fusion.2), kind=kOutput, calls=%fused_computation.61 | convolution fusion | flops 1207962624 | bytes 14680256 | tf_op jit(solution)/shard_map/dot_general | solution.py:127
  (115 shorter events, 1.7 us)
Async XLA Ops:
  7.2 61.5 %copy-start = (f32[1536]{0:T(1024)S(1)}, f32[1536]{0:T(1024)}, u32[]{:S(2)}) copy-start(f32[1536]{0:T(1024)} %param.15) | copy-start | bytes 18436
  23.9 12.3 %copy-start.1 = (f32[1536]{0:T(1024)S(1)}, f32[1536]{0:T(1024)}, u32[]{:S(2)}) copy-start(f32[1536]{0:T(1024)} %param.17) | copy-start | bytes 18436
  23.9 12.3 %copy-start.2 = (f32[1536]{0:T(1024)S(1)}, f32[1536]{0:T(1024)}, u32[]{:S(2)}) copy-start(f32[1536]{0:T(1024)} %param.18) | copy-start | bytes 18436
  23.9 12.3 %copy-start.4 = (f32[512]{0:T(512)S(1)}, f32[512]{0:T(512)}, u32[]{:S(2)}) copy-start(f32[512]{0:T(512)} %param.19) | copy-start | bytes 6148
  23.9 13.9 %copy-start.5 = (s32[1536]{0:T(1024)S(1)}, s32[1536]{0:T(1024)}, u32[]{:S(2)}) copy-start(s32[1536]{0:T(1024)} %param.16) | copy-start | bytes 18436
  31.7 40.5 %all-to-all-start = ((f32[4,24,4096]{2,1,0:T(8,128)}), f32[4,24,4096]{2,1,0:T(8,128)}, u32[]{:S(2)}, u32[]{:S(2)}) async-start(f32[4,24,4096]{2,1,0:T(8,128)} %bitcast.3), calls=%async_computation | async-start | bytes 3145728 | tf_op jit(solution)/shard_map/all_to_all | solution.py:65
  68.7 7.9 %slice-start = ((s8[6291456]{0:T(1024)(128)(4,1)}), s8[2097152]{0:T(1024)(128)(4,1)S(1)}, s32[]{:S(2)}) async-start(s8[6291456]{0:T(1024)(128)(4,1)} %bitcast.41), calls=%async_computation.4 | async-start | bytes 4194304
  72.2 4.3 %slice-start.1 = ((s8[6291456]{0:T(1024)(128)(4,1)}), s8[4194304]{0:T(1024)(128)(4,1)S(1)}, s32[]{:S(2)}) async-start(s8[6291456]{0:T(1024)(128)(4,1)} %bitcast.41), calls=%async_computation.5 | async-start | bytes 8388608
  83.1 9.1 %copy-start.3 = (f32[384,4096]{1,0:T(8,128)}, f32[384,4096]{1,0:T(8,128)S(1)}, u32[]{:S(2)}) copy-start(f32[384,4096]{1,0:T(8,128)S(1)} %multiply_add_fusion) | copy-start | bytes 18874372
  92.2 195.3 %all-to-all-start.1 = ((f32[32,16,4096]{2,1,0:T(8,128)}), f32[32,16,4096]{2,1,0:T(8,128)}, u32[]{:S(2)}, u32[]{:S(2)}) async-start(f32[32,16,4096]{2,1,0:T(8,128)} %bitcast.39), calls=%async_computation.1 | async-start | bytes 16777216 | tf_op jit(solution)/shard_map/all_to_all | solution.py:114
  100.1 197.1 %reduce-scatter.2.cloned.1.call-start = ((), (), s32[]{:S(2)}) async-start(), calls=%async_computation.3 | async-start | bytes 10485760 | tf_op jit(solution)/shard_map/reduce_scatter | solution.py:93
Sparse Core Ops, SparseCore 0:
  118.3 112.3 reduce-scatter.1
where the time goes:
time: 305 us; the launch traced here: 304 us
  waiting for transfers between devices  169 us (55%)
  matrix products  50.3 us (16%)
  local copies, waits for them, and re-layouts  38.8 us (13%)
  other arithmetic  18.9 us (6%)
  between operations  14.4 us (5%)
  starting transfers between devices  12.3 us (4%)
    all_to_all x1, waiting for transfers between devices, shards(): lax.all_to_all(parcels, ('row', 'col'), split_axis=0, concat_axis=0, tile...  169 us
    dot_general x4, matrix products, select_rows(): jnp.dot(pick, source, precision=lax.Precision.HIGHEST, preferred_element_...  26.4 us
    dot_general x1, matrix products, shards(): lax.dot_general(cauchy, spun_vectors, (((0,), (0,)), ((), ())), precision...  18 us
    gather x18, local copies, waits for them, and re-layouts, bucket_table(): edge_ids = jnp.searchsorted(sorted_keys, boundary_keys)  13 us
    all_to_all x1, starting transfers between devices, shards(): lax.all_to_all(parcels, ('row', 'col'), split_axis=0, concat_axis=0, tile...  7.92 us
    sort x2, other arithmetic, bucket_table(): ordering = jnp.argsort(sort_keys, stable=True)  7.54 us
  transfers between devices with their start and end apart: 3, of which 1 were waited for; matrix products, arithmetic and copies ran while one was open for 21% of the time, Pallas kernels for 0%

commit v1 on v0

v1 whole, which is shorter than its diff:
```python
import functools

import jax
import jax.numpy as jnp
from jax import lax
from jax.experimental import pallas as pl
from jax.experimental.pallas import tpu as pltpu
from jax.sharding import PartitionSpec as P

MESH = pl.DeviceIdType.MESH
CHUNKS = 8
AHEAD = 2


def dot(a, b):
    return jnp.dot(a, b, precision=lax.Precision.HIGHEST, preferred_element_type=jnp.float32)


def rolled(array, shift, axis):
    twice = jnp.concatenate([array, array], axis=axis)
    return lax.dynamic_slice_in_dim(twice, shift, array.shape[axis], axis)


def exchange(
    rows, cols, width,
    x_ref, give_ref, own_ref, mate_ref, place_ref, weight_ref,
    packed_ref, panel_ref,
    rot_out, rot_in, col_out, col_in, row_out, half_out, half_in, half_own, part_out, part_in,
    rot_send, rot_recv, col_send, col_recv, row_send, row_recv, half_send, half_recv,
    part_send, part_recv, self_sem,
):
    row, col = lax.axis_index("row"), lax.axis_index("col")
    chips = cols // 2
    chip, core = col // 2, lax.rem(col, 2)
    twin = chip * 2 + 1 - core
    span = x_ref.shape[1]
    every = packed_ref.shape[0]
    cap = col_in.shape[2]
    blk = panel_ref.shape[0]

    barrier = pltpu.get_barrier_semaphore()
    for o in range(1, cols):
        pl.semaphore_signal(
            barrier, inc=1, device_id=(row, lax.rem(col + o, cols)), device_id_type=MESH
        )
    for q in range(1, rows):
        pl.semaphore_signal(
            barrier, inc=1, device_id=(lax.rem(row + q, rows), col), device_id_type=MESH
        )
    pl.semaphore_wait(barrier, cols + rows - 2)

    def lanes(c):
        return pl.ds(pl.multiple_of(c * width, 128), width)

    def rot_copy(c, o):
        return pltpu.make_async_remote_copy(
            rot_out.at[c, o - 1], rot_in.at[c, o - 1],
            rot_send.at[c, o - 1], rot_recv.at[c, o - 1],
            device_id=(row, lax.rem(col + o, cols)), device_id_type=MESH,
        )

    def col_copy(c, o):
        return pltpu.make_async_remote_copy(
            col_out.at[c, o - 1], col_in.at[c, o],
            col_send.at[c, o - 1], col_recv.at[c, o - 1],
            device_id=(row, lax.rem(col + o, cols)), device_id_type=MESH,
        )

    def target(c, source_row):
        return packed_ref.at[:, pl.ds(pl.multiple_of(source_row * span + c * width, 128), width)]

    def row_copy(c, q):
        return pltpu.make_async_remote_copy(
            row_out.at[c, q], target(c, row),
            row_send.at[c, q - 1], row_recv.at[c, q - 1],
            device_id=(lax.rem(row + q, rows), col), device_id_type=MESH,
        )

    def row_arrival(c, q):
        return pltpu.make_async_remote_copy(
            row_out.at[c, q], target(c, lax.rem(row + rows - q, rows)),
            row_send.at[c, q - 1], row_recv.at[c, q - 1],
            device_id=(lax.rem(row + q, rows), col), device_id_type=MESH,
        )

    def self_copy(c):
        return pltpu.make_async_copy(row_out.at[c, 0], target(c, row), self_sem.at[c])

    def half_copy(c):
        return pltpu.make_async_remote_copy(
            half_out.at[c], half_in.at[c], half_send.at[c], half_recv.at[c],
            device_id=(row, twin), device_id_type=MESH,
        )

    def part_copy(c, o):
        return pltpu.make_async_remote_copy(
            part_out.at[c, o - 1], part_in.at[c, o - 1],
            part_send.at[c, o - 1], part_recv.at[c, o - 1],
            device_id=(row, lax.rem(chip + o, chips) * 2 + core), device_id_type=MESH,
        )

    def send_mates(c):
        found = dot(give_ref[...], x_ref[:, lanes(c)])
        rot_out[c] = found.reshape(rot_out.shape[1:])
        for o in range(1, cols):
            rot_copy(c, o).start()

    def send_rows(c):
        for o in range(1, cols):
            col_copy(c, o).wait_recv()
        found = dot(place_ref[...], col_in[c].reshape(cols * cap, width))
        row_out[c] = found.reshape(rows, every, width)
        for q in range(1, rows):
            row_copy(c, q).start()
        self_copy(c).start()

    def fold(c):
        half_copy(c).wait_recv()
        total = half_own[c] + half_in[c]
        panel_ref[:, lanes(c)] = total[:blk]
        part_out[c] = total[blk:].reshape(chips - 1, blk, width)

    def main(c, carry):
        for o in range(1, cols):
            rot_copy(c, o).wait_recv()
        here = x_ref[:, lanes(c)]
        mates = rot_in[c].reshape(rot_in.shape[1] * rot_in.shape[2], width)
        spun = dot(own_ref[...], here) + dot(mate_ref[...], mates)
        col_in[c, 0] = spun[:cap]
        col_out[c] = spun[cap:].reshape(cols - 1, cap, width)
        for o in range(1, cols):
            col_copy(c, o).start()

        @pl.when(c + AHEAD < CHUNKS)
        def _():
            send_mates(c + AHEAD)

        sums = dot(weight_ref[...], here)
        half_own[c] = sums[: chips * blk]
        half_out[c] = sums[chips * blk :]
        half_copy(c).start()

        @pl.when(c >= 1)
        def _():
            fold(c - 1)

        @pl.when(c >= AHEAD)
        def _():
            send_rows(c - AHEAD)

        return carry

    lax.fori_loop(0, AHEAD, lambda c, z: (send_mates(c), z)[1], 0)
    lax.fori_loop(0, CHUNKS, main, 0)
    fold(CHUNKS - 1)

    def send_parts(c, carry):
        for o in range(1, chips):
            part_copy(c, o).start()
        return carry

    lax.fori_loop(0, CHUNKS, send_parts, 0)
    lax.fori_loop(CHUNKS - AHEAD, CHUNKS, lambda c, z: (send_rows(c), z)[1], 0)

    def finish_panel(c, carry):
        total = panel_ref[:, lanes(c)]
        for o in range(1, chips):
            part_copy(c, o).wait_recv()
            total = total + part_in[c, o - 1]
        panel_ref[:, lanes(c)] = total
        for o in range(1, chips):
            part_copy(c, o).wait_send()
        half_copy(c).wait_send()
        for o in range(1, cols):
            rot_copy(c, o).wait_send()
            col_copy(c, o).wait_send()
        return carry

    lax.fori_loop(0, CHUNKS, finish_panel, 0)

    def finish_rows(c, carry):
        for q in range(1, rows):
            row_arrival(c, q).wait_recv()
            row_copy(c, q).wait_send()
        self_copy(c).wait()
        return carry

    lax.fori_loop(0, CHUNKS, finish_rows, 0)


def shards(
    eigvec_halves,
    rotation_mate,
    givens_theta,
    kept_vectors,
    secular_singularities,
    secular_coefficients,
    secular_zeros,
):
    cols = lax.axis_size("col")
    rows = lax.axis_size("row")
    block, span = eigvec_halves.shape
    total_cols = rotation_mate.shape[0]
    panel_cols = secular_zeros.shape[0]
    pair_cap = block // 16
    chips = cols // 2
    blk = panel_cols // cols
    every = block // rows
    share = every // cols
    cap = rows * (share + share // 3)
    width = span // CHUNKS
    col, row = lax.axis_index("col"), lax.axis_index("row")
    first = col * block
    ids = jnp.arange(block, dtype=jnp.int32)
    labels = first + ids
    mate = lax.dynamic_slice_in_dim(rotation_mate, first, block)
    paired = mate != labels
    owner = mate // block
    remote = paired & (owner != col)

    def count(mask):
        return jnp.sum(mask.astype(jnp.int32), axis=0)

    same = (owner[:, None] == owner[None, :]) & remote[:, None]
    rank_out = count(same & (mate[:, None] < mate[None, :]))
    rank_in = count(same & (ids[:, None] < ids[None, :]))
    slot_out = jnp.where(remote, ((owner - col + cols) % cols - 1) * pair_cap + rank_out, -1)
    slot_in = jnp.where(remote, ((col - owner + cols) % cols - 1) * pair_cap + rank_in, -1)
    pair_slots = jnp.arange((cols - 1) * pair_cap, dtype=jnp.int32)
    give = (pair_slots[:, None] == slot_out[None, :]).astype(jnp.float32)

    every_id = jnp.arange(total_cols, dtype=jnp.int32)

    def lookup(mask, values):
        return jnp.sum(jnp.where(mask, values[:, None], jnp.zeros((), values.dtype)), axis=0)

    mine = kept_vectors[:, None] == labels[None, :]
    theirs = kept_vectors[:, None] == mate[None, :]
    spot, spot_mate = lookup(mine, every_id), lookup(theirs, every_id)
    pole, pole_mate = lookup(mine, secular_singularities), lookup(theirs, secular_singularities)
    weight, weight_mate = lookup(mine, secular_coefficients), lookup(theirs, secular_coefficients)
    angle = lookup(every_id[:, None] == jnp.minimum(labels, mate)[None, :], givens_theta)
    cosine = jnp.where(paired, jnp.cos(angle), 1.0)
    sine = jnp.where(paired, jnp.where(labels < mate, -1.0, 1.0) * jnp.sin(angle), 0.0)

    goal, goal_mate = (spot // every) % cols, (spot_mate // every) % cols

    def move_slot(goals, spots):
        before = (goal[:, None] == goals[None, :]) & (spot[:, None] < spots[None, :])
        return ((goals - col + cols) % cols) * cap + count(before)

    slot, slot_mate = move_slot(goal, spot), move_slot(goal_mate, spot_mate)
    move_slots = jnp.arange(cols * cap, dtype=jnp.int32)
    local = paired & jnp.logical_not(remote)
    own = jnp.where(move_slots[:, None] == slot[None, :], cosine[None, :], 0.0) + jnp.where(
        (move_slots[:, None] == slot_mate[None, :]) & local[None, :], -sine[None, :], 0.0
    )
    taken = slot_in[:, None] == pair_slots[None, :]
    from_slot, from_sine = lookup(taken, slot), lookup(taken, sine)
    from_mate = jnp.where(move_slots[:, None] == from_slot[None, :], from_sine[None, :], 0.0)

    wanted = lax.dynamic_index_in_dim(
        kept_vectors.reshape(rows, cols, every), col, 1, keepdims=False
    ).reshape(-1)
    source = wanted // block
    rank = count((source[:, None] == source[None, :]) & (ids[:, None] < ids[None, :]))
    arrived = ((col - source + cols) % cols) * cap + rank
    arrived = rolled(arrived.reshape(rows, every), row, 0).reshape(-1)
    place = (arrived[:, None] == move_slots[None, :]).astype(jnp.float32)

    raw = secular_coefficients[:, None] / (
        secular_singularities[:, None] - secular_zeros[None, :]
    )
    scale = lax.rsqrt(jnp.sum(raw * raw, axis=0) + 1e-06)

    def ordered(array):
        parts = rolled(array.reshape(chips, 2, blk), col // 2, 0)
        return rolled(parts, col % 2, 1).transpose(1, 0, 2).reshape(-1)

    zeros, scale = ordered(secular_zeros), ordered(scale)
    cauchy = weight[None, :] / (pole[None, :] - zeros[:, None])
    cauchy_mate = weight_mate[None, :] / (pole_mate[None, :] - zeros[:, None])
    weights = (cosine[None, :] * cauchy - sine[None, :] * cauchy_mate) * scale[:, None]

    vmem = pl.BlockSpec(memory_space=pltpu.VMEM)
    f32 = jnp.float32
    dma = pltpu.SemaphoreType.DMA
    return pl.pallas_call(
        functools.partial(exchange, rows, cols, width),
        out_shape=(
            jax.ShapeDtypeStruct((every, rows * span), f32),
            jax.ShapeDtypeStruct((blk, span), f32),
        ),
        in_specs=[vmem] * 6,
        out_specs=(pl.BlockSpec(memory_space=pl.ANY), vmem),
        scratch_shapes=[
            pltpu.VMEM((CHUNKS, cols - 1, pair_cap, width), f32),
            pltpu.VMEM((CHUNKS, cols - 1, pair_cap, width), f32),
            pltpu.VMEM((CHUNKS, cols - 1, cap, width), f32),
            pltpu.VMEM((CHUNKS, cols, cap, width), f32),
            pltpu.VMEM((CHUNKS, rows, every, width), f32),
            pltpu.VMEM((CHUNKS, chips * blk, width), f32),
            pltpu.VMEM((CHUNKS, chips * blk, width), f32),
            pltpu.VMEM((CHUNKS, chips * blk, width), f32),
            pltpu.VMEM((CHUNKS, chips - 1, blk, width), f32),
            pltpu.VMEM((CHUNKS, chips - 1, blk, width), f32),
            dma((CHUNKS, cols - 1)), dma((CHUNKS, cols - 1)),
            dma((CHUNKS, cols - 1)), dma((CHUNKS, cols - 1)),
            dma((CHUNKS, rows - 1)), dma((CHUNKS, rows - 1)),
            dma((CHUNKS,)), dma((CHUNKS,)),
            dma((CHUNKS, chips - 1)), dma((CHUNKS, chips - 1)),
            dma((CHUNKS,)),
        ],
        compiler_params=pltpu.CompilerParams(
            collective_id=0, has_side_effects=True, vmem_limit_bytes=60 * 1024 * 1024
        ),
    )(eigvec_halves, give, own, from_mate, place, weights)


def solution(mesh):
    placed = (P("col", "row"), P(), P(), P(), P(), P(), P())
    return jax.shard_map(
        shards,
        mesh=mesh,
        in_specs=placed,
        out_specs=(P(("row", "col"), None), P("col", "row")),
        check_vma=False,
    )
```

time: 305 us -> 200 us (0.66)
  the two profiles are of different devices: /device:TPU:0 before, /device:TPU:15 now
where the time goes in v1:
time: 200 us
  Pallas kernels  176 us (88%)
  other arithmetic  13.4 us (7%)
  local copies, waits for them, and re-layouts  8.99 us (4%)
    pallas_call x1, Pallas kernels, shards(): pl.pallas_call(functools.partial(exchange, rows, cols, width), out_shape=...  176 us
    unnamed x4, local copies, waits for them, and re-layouts  7.36 us
    reduce_sum x5, other arithmetic, lookup(): jnp.sum(jnp.where(mask, values[:, None], jnp.zeros((), values.dtype)), ax...  4.67 us

profile of v1, /device:TPU:15, one launch (start us, length us, event | category | flops | bytes accessed | tf_op | source)
XLA Modules:
  0.0 199.5 jit_solution(9532593127427546147)
XLA Ops:
  0.7 0.7 fusion.42
  1.4 1.3 multiply_reduce_fusion
  2.8 0.8 not_and_fusion
  3.6 0.3 convert_reduce_fusion.1
  3.9 1.0 select_reduce_fusion
  5.0 0.1 select_reduce_fusion.1
  5.1 1.3 fusion
  6.4 0.3 convert_reduce_fusion.3
  6.7 0.1 select_reduce_fusion.2
  6.8 2.2 %fusion.2 = (f32[384]{0:T(512)S(1)}, f32[384]{0:T(512)S(1)}, f32[384]{0:T(512)S(1)}, f32[384]{0:T(512)S(1)}) fusion(f32[1536]{0:T(1024)} %param.11, s32[384]{0:T(512)S(1)} %iota_add_fusion, s32[1536]{0:T(1024)} %param.10, s32[384]{0:T(512)S(1)} %get-tuple-element.21, f32[1536]{0:T(1024)} %param.12), kind=kLoop, calls=%fused_computation.9 | loop fusion | flops 5896704 | bytes 27648 | tf_op jit(solution)/shard_map/reduce_sum | solution.py:235
  9.0 0.8 reshape.231
  9.7 0.5 broadcast.478
  10.3 1.0 fusion.49
  11.3 0.1 div.92
  11.4 0.1 and.211
  11.5 0.1 convert_reduce_fusion
  11.6 0.1 reduce_sum.147
  11.8 0.1 eq.209
  11.8 0.7 fusion.11.give_ref
  12.5 0.8 fusion.10.mate_ref
  13.3 1.1 fusion.7.place_ref
  14.3 1.5 subtract_multiply_fusion
  15.8 176.3 %shard_map.86 = (f32[48,32768]{1,0:T(8,128)}, f32[128,4096]{1,0:T(8,128)}) custom-call(f32[384,4096]{1,0:T(8,128)} %x_ref.1, f32[72,384]{1,0:T(8,128)} %fusion.11.give_ref, f32[512,384]{1,0:T(8,128)} %get-tuple-element.28.own_ref, f32[512,72]{1,0:T(8,128)} %fusion.10.mate_ref, f32[384,512]{1,0:T(8,128)} %fusion.7.place_ref, ...), custom_call_target="tpu_custom_call" | custom-call | tf_op jit(solution)/shard_map/pallas_call | solution.py:288
  192.1 0.0 copy-start
  192.1 6.0 %copy.24 = f32[48,32768]{1,0:T(8,128)} copy(f32[48,32768]{1,0:T(8,128)} %get-tuple-element.36) | data formatting | bytes 12582912
  198.2 0.0 copy-done
  198.2 1.3 copy.25
  (16 shorter events, 0.3 us)
Async XLA Ops:
  192.1 6.1 %copy-start = (f32[128,4096]{1,0:T(8,128)S(1)}, f32[128,4096]{1,0:T(8,128)}, u32[]{:S(2)}) copy-start(f32[128,4096]{1,0:T(8,128)} %get-tuple-element.37) | copy-start | bytes 6291460

commit v2 on v1

--- a/solution.py
+++ b/solution.py
@@ -8,7 +8,7 @@
 from jax.sharding import PartitionSpec as P
 
 MESH = pl.DeviceIdType.MESH
-CHUNKS = 8
+CHUNKS = 16
 AHEAD = 2
 
 
@@ -135,6 +135,10 @@
         def _():
             send_mates(c + AHEAD)
 
+        @pl.when(c >= AHEAD)
+        def _():
+            send_rows(c - AHEAD)
+
         sums = dot(weight_ref[...], here)
         half_own[c] = sums[: chips * blk]
         half_out[c] = sums[chips * blk :]
@@ -143,10 +147,6 @@
         @pl.when(c >= 1)
         def _():
             fold(c - 1)
-
-        @pl.when(c >= AHEAD)
-        def _():
-            send_rows(c - AHEAD)
 
         return carry
 
@@ -288,11 +288,11 @@
     return pl.pallas_call(
         functools.partial(exchange, rows, cols, width),
         out_shape=(
-            jax.ShapeDtypeStruct((every, rows * span), f32),
-            jax.ShapeDtypeStruct((blk, span), f32),
+            pltpu.VMEM((every, rows * span), f32),
+            pltpu.VMEM((blk, span), f32),
         ),
         in_specs=[vmem] * 6,
-        out_specs=(pl.BlockSpec(memory_space=pl.ANY), vmem),
+        out_specs=(vmem, vmem),
         scratch_shapes=[
             pltpu.VMEM((CHUNKS, cols - 1, pair_cap, width), f32),
             pltpu.VMEM((CHUNKS, cols - 1, pair_cap, width), f32),
@@ -312,7 +312,7 @@
             dma((CHUNKS,)),
         ],
         compiler_params=pltpu.CompilerParams(
-            collective_id=0, has_side_effects=True, vmem_limit_bytes=60 * 1024 * 1024
+            collective_id=0, has_side_effects=True, vmem_limit_bytes=54 * 1024 * 1024
         ),
     )(eigvec_halves, give, own, from_mate, place, weights)
 

time: 200 us -> 191 us (0.955)
  the two profiles are of different devices: /device:TPU:15 before, /device:TPU:0 now
where the time goes in v2:
time: 191 us; the launch traced here: 190 us
  Pallas kernels  171 us (90%)
  other arithmetic  13.3 us (7%)
  local copies, waits for them, and re-layouts  5.65 us (3%)
    pallas_call x1, Pallas kernels, shards(): pl.pallas_call(functools.partial(exchange, rows, cols, width), out_shape=...  171 us
    reduce_sum x5, other arithmetic, lookup(): jnp.sum(jnp.where(mask, values[:, None], jnp.zeros((), values.dtype)), ax...  4.67 us
    unnamed x2, local copies, waits for them, and re-layouts  4.02 us

profile of v2, /device:TPU:0, one launch (start us, length us, event | category | flops | bytes accessed | tf_op | source)
XLA Modules:
  0.0 190.3 jit_solution(14849204722453328915)
XLA Ops:
  0.7 0.7 fusion.42
  1.4 1.3 multiply_reduce_fusion
  2.8 0.8 not_and_fusion
  3.6 0.3 convert_reduce_fusion.1
  3.9 1.0 select_reduce_fusion
  5.0 0.1 select_reduce_fusion.1
  5.1 1.3 fusion
  6.4 0.3 convert_reduce_fusion.3
  6.7 0.1 select_reduce_fusion.2
  6.8 2.2 %fusion.2 = (f32[384]{0:T(512)S(1)}, f32[384]{0:T(512)S(1)}, f32[384]{0:T(512)S(1)}, f32[384]{0:T(512)S(1)}) fusion(f32[1536]{0:T(1024)} %param.11, s32[384]{0:T(512)S(1)} %iota_add_fusion, s32[1536]{0:T(1024)} %param.10, s32[384]{0:T(512)S(1)} %get-tuple-element.21, f32[1536]{0:T(1024)} %param.12), kind=kLoop, calls=%fused_computation.9 | loop fusion | flops 5896704 | bytes 27648 | tf_op jit(solution)/shard_map/reduce_sum | solution.py:235
  9.0 0.8 reshape.231
  9.7 0.5 broadcast.478
  10.3 1.0 fusion.49
  11.3 0.1 div.92
  11.4 0.1 and.211
  11.5 0.1 convert_reduce_fusion
  11.6 0.1 reduce_sum.147
  11.8 0.1 eq.209
  11.8 0.7 fusion.11.give_ref
  12.5 0.7 fusion.10.mate_ref
  13.2 1.0 fusion.7.place_ref
  14.2 1.5 subtract_multiply_fusion
  15.7 170.6 %shard_map.86 = (f32[48,32768]{1,0:T(8,128)S(1)}, f32[128,4096]{1,0:T(8,128)S(1)}) custom-call(f32[384,4096]{1,0:T(8,128)} %x_ref.1, f32[72,384]{1,0:T(8,128)} %fusion.11.give_ref, f32[512,384]{1,0:T(8,128)} %get-tuple-element.28.own_ref, f32[512,72]{1,0:T(8,128)} %fusion.10.mate_ref, f32[384,512]{1,0:T(8,128)} %fusion.7.place_ref, ...), custom_call_target="tpu_custom_call" | custom-call | tf_op jit(solution)/shard_map/pallas_call | solution.py:288
  186.3 2.7 %copy.24 = f32[48,32768]{1,0:T(8,128)} copy(f32[48,32768]{1,0:T(8,128)S(1)} %get-tuple-element.34) | data formatting | bytes 12582912
  189.0 1.3 copy.25
  (16 shorter events, 0.3 us)
